TPU v7x, 32 devices: a whole 2x2x4 slice. The times are simulated.
32 devices in a mesh: bank: 4 (over x, core), zero: 8 (over z, y).
Axes of the slice: x: 2, y: 2, z: 4, core: 2. Of those that a mesh axis runs over, the one named last changes fastest.
Arguments:
- train_gate: float32 [128, 2048, 768], P('bank', 'zero'), may hold values from -0.1875 to 0.1875
- other_gate: bfloat16 [128, 2048, 768], P('bank', 'zero'), may hold values from -0.0625 to 0.0625
- train_up: float32 [128, 2048, 768], P('bank', 'zero'), may hold values from -0.1875 to 0.1875
- other_up: bfloat16 [128, 2048, 768], P('bank', 'zero'), may hold values from -0.0625 to 0.0625
- router_weight: float32 [2048, 128], P('zero', 'bank'), may hold values from -0.125 to 0.125
- router_gain: float32 [2048], P('zero'), may hold values from 0.25 to 1.75
Outputs:
- ready_gate: bfloat16 [128, 2048, 768], P('bank', None, 'zero')
- ready_up: bfloat16 [128, 2048, 768], P('bank', None, 'zero')
- scale_gate: float32 [128, 768], P('bank', 'zero')
- scale_up: float32 [128, 768], P('bank', 'zero')
- serve_router: bfloat16 [2048, 128], replicated
All inputs are finite; a program needn't handle non-finite values. Where the computation divides by a largest or mean magnitude, that divisor is 1e-20 or more.
Results may differ from a plain program's by a relative error of at most 0.001.
Values may be sent and summed in bfloat16 or wider, within the bound.
A program may use at most 256 MiB of HBM per device.

v0:
```python
import jax
import jax.numpy as jnp
from jax import lax
from jax.sharding import PartitionSpec as P


def on_device(train_gate, other_gate, train_up, other_up, router_weight, router_gain):
    latest_gate = train_gate + other_gate.astype(jnp.float32)
    latest_up = train_up + other_up.astype(jnp.float32)
    scale_gate, scale_up = lax.pmax(
        (jnp.max(jnp.abs(latest_gate), axis=1), jnp.max(jnp.abs(latest_up), axis=1)), "zero"
    )
    narrow_gate, narrow_up = (
        (latest_gate / jnp.expand_dims(scale_gate, 1)).astype(jnp.bfloat16),
        (latest_up / jnp.expand_dims(scale_up, 1)).astype(jnp.bfloat16),
    )
    ready_gate, ready_up = (
        lax.all_to_all(narrow_gate, "zero", split_axis=2, concat_axis=1, tiled=True),
        lax.all_to_all(narrow_up, "zero", split_axis=2, concat_axis=1, tiled=True),
    )
    scale_gate = lax.dynamic_slice_in_dim(
        scale_gate, lax.axis_index("zero") * ready_gate.shape[2], ready_gate.shape[2], axis=1
    )
    scale_up = lax.dynamic_slice_in_dim(
        scale_up, lax.axis_index("zero") * ready_up.shape[2], ready_up.shape[2], axis=1
    )
    part_router = (router_weight * router_gain[:, None]).astype(jnp.bfloat16)
    row_router = lax.all_gather(part_router, "zero", axis=0, tiled=True)
    serve_router = lax.all_gather(row_router, "bank", axis=1, tiled=True)
    return (ready_gate, ready_up, scale_gate, scale_up, serve_router)


def solution(mesh):
    return jax.shard_map(
        on_device,
        mesh=mesh,
        in_specs=(
            P("bank", "zero", None),
            P("bank", "zero", None),
            P("bank", "zero", None),
            P("bank", "zero", None),
            P("zero", "bank"),
            P("zero"),
        ),
        out_specs=(
            P("bank", None, "zero"),
            P("bank", None, "zero"),
            P("bank", "zero"),
            P("bank", "zero"),
            P(),
        ),
        check_vma=False,
    )
```

profile of v0, /device:TPU:0, one launch (start us, length us, event | category | flops | bytes accessed | tf_op | source)
XLA Modules:
  0.0 885.5 jit_solution(4941322030642369728)
XLA Ops:
  7.2 0.0 all-reduce.3.cloned.1.call-start
  7.2 25.0 %copy.42 = f32[32,256,768]{1,0,2:T(8,128)} copy(f32[32,256,768]{2,1,0:T(8,128)} %param.8) | data formatting | bytes 50331648 | tf_op args[2]
  32.2 16.9 %copy.41 = bf16[32,256,768]{1,0,2:T(8,128)(2,1)} copy(bf16[32,256,768]{2,1,0:T(8,128)(2,1)} %param.9) | data formatting | bytes 25165824 | tf_op args[3]
  49.1 25.0 %copy.38 = f32[32,256,768]{1,0,2:T(8,128)} copy(f32[32,256,768]{2,1,0:T(8,128)} %param.6) | data formatting | bytes 50331648 | tf_op args[0]
  74.2 16.9 %copy.37 = bf16[32,256,768]{1,0,2:T(8,128)(2,1)} copy(bf16[32,256,768]{2,1,0:T(8,128)(2,1)} %param.7) | data formatting | bytes 25165824 | tf_op args[1]
  91.0 0.0 copy-start
  91.0 14.4 %abs_reduce_fusion = f32[32,768]{0,1:T(8,128)} fusion(f32[32,256,768]{1,0,2:T(8,128)} %copy.42, bf16[32,256,768]{1,0,2:T(8,128)(2,1)} %copy.41), kind=kLoop, calls=%fused_computation.1 | loop fusion | flops 25141248 | bytes 37847040 | tf_op jit(solution)/shard_map/reduce_max | solution.py:11
  105.4 4.7 copy-done
  110.1 9.7 %abs_reduce_fusion.1 = f32[32,768]{0,1:T(8,128)} fusion(f32[32,256,768]{1,0,2:T(8,128)S(1)} %copy-done, bf16[32,256,768]{1,0,2:T(8,128)(2,1)} %copy.37), kind=kLoop, calls=%fused_computation.4 | loop fusion | flops 25141248 | bytes 37847040 | tf_op jit(solution)/shard_map/reduce_max | solution.py:11
  119.9 0.0 all-reduce.3.cloned.1.call-update
  119.9 78.2 %all-reduce.3.cloned.1.call-done = (f32[32,768]{0,1:T(8,128)}, f32[32,768]{0,1:T(8,128)}) async-done(((f32[32,768]{0,1:T(8,128)}, f32[32,768]{0,1:T(8,128)}), (f32[32,768]{0,1:T(8,128)}, f32[32,768]{0,1:T(8,128)})) %all-reduce.3.cloned.1.call-update) | async-done | bytes 196624 | tf_op jit(solution)/shard_map/pmax | solution.py:10
  198.1 29.4 %divide_convert_fusion = (bf16[32,256,768]{1,0,2:T(8,128)(2,1)}, bf16[32,256,768]{1,0,2:T(8,128)(2,1)S(1)}) fusion(f32[32,256,768]{1,0,2:T(8,128)} %copy.42, bf16[32,256,768]{1,0,2:T(8,128)(2,1)} %copy.41, f32[32,768]{0,1:T(8,128)} %get-tuple-element.16, f32[32,768]{0,1:T(8,128)} %get-tuple-element.15, f32[32,256,768]{1,0,2:T(8,128)} %copy.38, ...), kind=kLoop, calls=%fused_computation | loop fusion | flops 50331648 | bytes 100859904 | tf_op jit(solution)/shard_map/convert_element_type | solution.py:15
  227.5 0.0 copy-start.1
  227.6 0.0 copy-start.2
  227.6 276.4 %all_to_all.36 = bf16[32,256,768]{1,0,2:T(8,128)(2,1)} all-to-all(bf16[32,256,768]{1,0,2:T(8,128)(2,1)S(1)} %get-tuple-element.18), channel_id=1, replica_groups=mesh['bank'=4,'zero'=8] {'zero'}, dimensions={2} | all-to-all | bytes 25165824 | tf_op jit(solution)/shard_map/all_to_all | solution.py:18
  504.0 5.4 all-to-all-start.1
  509.3 0.0 copy-done.1
  509.4 0.0 copy-done.2
  509.4 292.0 %all_gather.6 = bf16[2048,32]{0,1:T(8,128)(2,1)S(1)} all-gather(bf16[256,32]{0,1:T(8,128)(2,1)S(1)} %multiply_convert_fusion), channel_id=1, replica_groups=mesh['bank'=4,'zero'=8] {'zero'}, dimensions={0}, use_global_device_ids=true | all-gather | bytes 147456 | tf_op jit(solution)/shard_map/all_gather | solution.py:28
  801.4 7.0 all_gather.7
  808.4 1.0 copy.47
  809.4 0.8 constant_dynamic-slice_fusion
  810.2 0.7 copy.45
  810.9 0.7 copy.46
  811.6 14.1 %copy.40 = bf16[32,8,256,96]{2,1,3,0:T(8,128)(2,1)} copy(bf16[32,8,256,96]{2,0,3,1:T(8,128)(2,1)} %bitcast.14) | data formatting | bytes 25165824 | tf_op jit(solution)/shard_map/all_to_all | solution.py:18
  825.6 19.5 %all_to_all.29 = bf16[32,2048,96]{1,2,0:T(8,128)(2,1)} reshape(bf16[32,8,256,96]{2,1,3,0:T(8,128)(2,1)} %copy.40) | data formatting | bytes 25165824 | tf_op jit(solution)/shard_map/all_to_all | solution.py:18
  845.1 0.0 all-to-all-done.1
  845.1 14.1 %copy.44 = bf16[32,8,256,96]{2,1,3,0:T(8,128)(2,1)} copy(bf16[32,8,256,96]{2,0,3,1:T(8,128)(2,1)} %bitcast.5) | data formatting | bytes 25165824 | tf_op jit(solution)/shard_map/all_to_all | solution.py:19
  859.2 19.5 %all_to_all.33 = bf16[32,2048,96]{1,2,0:T(8,128)(2,1)} reshape(bf16[32,8,256,96]{2,1,3,0:T(8,128)(2,1)} %copy.44) | data formatting | bytes 25165824 | tf_op jit(solution)/shard_map/all_to_all | solution.py:19
  (1 shorter events, 0.0 us)
Async XLA Ops:
  7.2 191.0 %all-reduce.3.cloned.1.call-start = ((), (), s32[]{:S(2)}) async-start(), calls=%async_computation.2 | async-start | bytes 1572864 | tf_op jit(solution)/shard_map/pmax | solution.py:10
  91.0 19.1 %copy-start = (f32[32,256,768]{1,0,2:T(8,128)S(1)}, f32[32,256,768]{1,0,2:T(8,128)}, u32[]{:S(2)}) copy-start(f32[32,256,768]{1,0,2:T(8,128)} %copy.38) | copy-start | bytes 75497472
  227.5 281.8 %copy-start.1 = (f32[256,32]{0,1:T(8,128)S(1)}, f32[256,32]{0,1:T(8,128)}, u32[]{:S(2)}) copy-start(f32[256,32]{0,1:T(8,128)} %param.10) | copy-start | bytes 98308
  227.6 281.8 %copy-start.2 = (f32[256]{0:T(256)S(1)}, f32[256]{0:T(256)}, u32[]{:S(2)}) copy-start(f32[256]{0:T(256)} %param.11) | copy-start | bytes 3076
  504.0 341.1 %all-to-all-start.1 = ((bf16[32,256,768]{1,0,2:T(8,128)(2,1)}), bf16[32,256,768]{1,0,2:T(8,128)(2,1)}, u32[]{:S(2)}, u32[]{:S(2)}) async-start(bf16[32,256,768]{1,0,2:T(8,128)(2,1)} %get-tuple-element.17), calls=%async_computation.1 | async-start | bytes 25165824 | tf_op jit(solution)/shard_map/all_to_all | solution.py:19
Sparse Core Ops, SparseCore 0:
  120.0 78.0 all-reduce.2
where the time goes:
time: 889 us; the launch traced here: 886 us
  blocking collectives  575 us (65%)
  local copies, waits for them, and re-layouts  159 us (18%)
  waiting for transfers between devices  78.2 us (9%)
  other arithmetic  53.5 us (6%)
  between operations  14.1 us (2%)
    all_gather x1, blocking collectives, on_device(): row_router = lax.all_gather(part_router, 'zero', axis=0, tiled=True)  292 us
    all_to_all x1, blocking collectives, on_device(): lax.all_to_all(narrow_gate, 'zero', split_axis=2, concat_axis=1, tiled=True)  276 us
    unnamed x13, local copies, waits for them, and re-layouts  90.9 us
    pmax x1, waiting for transfers between devices, on_device(): lax.pmax((jnp.max(jnp.abs(latest_gate), axis=1), jnp.max(jnp.abs(latest_u...  78.2 us
    all_to_all x2, local copies, waits for them, and re-layouts, on_device(): lax.all_to_all(narrow_gate, 'zero', split_axis=2, concat_axis=1, tiled=True)  33.5 us
    all_to_all x2, local copies, waits for them, and re-layouts, on_device(): lax.all_to_all(narrow_up, 'zero', split_axis=2, concat_axis=1, tiled=True)  33.5 us
    convert_element_type x1, other arithmetic, on_device(): (latest_up / jnp.expand_dims(scale_up, 1)).astype(jnp.bfloat16)  29.4 us
  transfers between devices with their start and end apart: 2, of which 1 were waited for; matrix products, arithmetic and copies ran while one was open for 2% of the time, Pallas kernels for 0%

commit v1 on v0

--- a/solution.py
+++ b/solution.py
@@ -1,10 +1,175 @@
+import functools
+
 import jax
 import jax.numpy as jnp
 from jax import lax
+from jax.experimental import pallas as pl
+from jax.experimental.pallas import tpu as pltpu
 from jax.sharding import PartitionSpec as P
 
-
-def on_device(train_gate, other_gate, train_up, other_up, router_weight, router_gain):
+LANES = 128
+SLOTS = 3
+
+
+def exchange(
+    n, held,
+    train_gate, other_gate, train_up, other_up,
+    ready_gate, ready_up, scale_ref,
+    train_in, other_in, stage, local_max, peer_max,
+    in_sem, own_sem, send_sem, recv_sem, max_send, max_recv,
+):
+    trains, others, readies = (train_gate, train_up), (other_gate, other_up), (ready_gate, ready_up)
+    experts, rows, width = train_gate.shape
+    piece = width // n
+    groups = experts // held
+    me = lax.axis_index("zero")
+    offsets = sorted(range(1, n), key=lambda k: abs(2 * k - n))
+
+    def loads(g):
+        slot = lax.rem(g, SLOTS)
+        some = pl.ds(g * held, held)
+        out = []
+        for t in range(2):
+            out.append(pltpu.make_async_copy(trains[t].at[some], train_in.at[slot, t], in_sem.at[slot, t, 0]))
+            out.append(pltpu.make_async_copy(others[t].at[some], other_in.at[slot, t], in_sem.at[slot, t, 1]))
+        return out
+
+    def max_copy(g, k):
+        return pltpu.make_async_remote_copy(
+            src_ref=local_max.at[g],
+            dst_ref=peer_max.at[g, k - 1],
+            send_sem=max_send.at[k - 1],
+            recv_sem=max_recv.at[g],
+            device_id={"zero": lax.rem(me + k, n)},
+            device_id_type=pl.DeviceIdType.MESH,
+        )
+
+    def find_max(g):
+        slot = lax.rem(g, SLOTS)
+        for copy in loads(g):
+            copy.wait()
+
+        for t in range(2):
+            for i in range(held):
+                for at in range(0, width, LANES):
+                    cols = pl.ds(at, LANES)
+                    latest = train_in[slot, t, i, :, cols] + other_in[slot, t, i, :, cols].astype(jnp.float32)
+                    local_max[g, t, i:i + 1, cols] = jnp.max(jnp.abs(latest), axis=0, keepdims=True)
+        for k in offsets:
+            max_copy(g, k).start()
+
+    def mine(ref):
+        return ref.at[:, :, pl.ds(pl.multiple_of(me * rows, LANES), rows)]
+
+    def scale_and_send(g):
+        slot = lax.rem(g, SLOTS)
+        pltpu.make_async_copy(peer_max.at[g], peer_max.at[g], max_recv.at[g]).wait()
+
+        for t in range(2):
+            scales = local_max[g, t]
+            for k in range(n - 1):
+                scales = jnp.maximum(scales, peer_max[g, k, t])
+            scale_ref[g, t] = scales
+            inverses = 1.0 / scales
+            for i in range(held):
+                inverse = inverses[i:i + 1, :]
+                for at in range(0, width, LANES):
+                    cols = pl.ds(at, LANES)
+                    latest = train_in[slot, t, i, :, cols] + other_in[slot, t, i, :, cols].astype(jnp.float32)
+                    narrow = (latest * inverse[:, at:at + LANES]).astype(jnp.bfloat16)
+                    stage[t, g * held + i, cols, :] = narrow.T
+        some = pl.ds(g * held, held)
+        for k in offsets:
+            to = lax.rem(me + k, n)
+            for t in range(2):
+                pltpu.make_async_remote_copy(
+                    src_ref=stage.at[t, some, pl.ds(pl.multiple_of(to * piece, 16), piece), :],
+                    dst_ref=mine(readies[t]).at[some],
+                    send_sem=send_sem.at[t, k - 1],
+                    recv_sem=recv_sem.at[t, k - 1],
+                    device_id={"zero": to},
+                    device_id_type=pl.DeviceIdType.MESH,
+                ).start()
+        for t in range(2):
+            pltpu.make_async_copy(
+                stage.at[t, some, pl.ds(pl.multiple_of(me * piece, 16), piece), :],
+                mine(readies[t]).at[some],
+                own_sem.at[t],
+            ).start()
+
+    for g in range(min(SLOTS, groups)):
+        for copy in loads(g):
+            copy.start()
+    barrier = pltpu.get_barrier_semaphore()
+    for k in offsets:
+        pl.semaphore_signal(
+            barrier, inc=1, device_id={"zero": lax.rem(me + k, n)}, device_id_type=pl.DeviceIdType.MESH
+        )
+    pl.semaphore_wait(barrier, n - 1)
+    find_max(0)
+
+    def step(g, carry):
+        @pl.when(g + 1 < groups)
+        def _():
+            find_max(g + 1)
+
+        scale_and_send(g)
+
+        @pl.when(g + SLOTS < groups)
+        def _():
+            for copy in loads(g + SLOTS):
+                copy.start()
+
+        return carry
+
+    lax.fori_loop(0, groups, step, 0)
+
+    for k in offsets:
+        sent = local_max
+        pltpu.make_async_copy(sent, sent, max_send.at[k - 1]).wait()
+        to, source = lax.rem(me + k, n), lax.rem(me + n - k, n)
+        for t in range(2):
+            sent = stage.at[t, :, pl.ds(pl.multiple_of(to * piece, 16), piece), :]
+            pltpu.make_async_copy(sent, sent, send_sem.at[t, k - 1]).wait()
+            got = readies[t].at[:, :, pl.ds(pl.multiple_of(source * rows, LANES), rows)]
+            pltpu.make_async_copy(got, got, recv_sem.at[t, k - 1]).wait()
+    for t in range(2):
+        pltpu.make_async_copy(mine(readies[t]), mine(readies[t]), own_sem.at[t]).wait()
+
+
+def weights_by_kernel(n, held, train_gate, other_gate, train_up, other_up):
+    experts, rows, width = train_gate.shape
+    piece, groups = width // n, experts // held
+    anywhere = pl.BlockSpec(memory_space=pltpu.MemorySpace.HBM)
+    ready = jax.ShapeDtypeStruct((experts, piece, n * rows), jnp.bfloat16)
+    ready_gate, ready_up, scales = pl.pallas_call(
+        functools.partial(exchange, n, held),
+        out_shape=(ready, ready, jax.ShapeDtypeStruct((groups, 2, held, width), jnp.float32)),
+        in_specs=[anywhere] * 4,
+        out_specs=(anywhere, anywhere, pl.BlockSpec(memory_space=pltpu.VMEM)),
+        scratch_shapes=[
+            pltpu.VMEM((SLOTS, 2, held, rows, width), jnp.float32),
+            pltpu.VMEM((SLOTS, 2, held, rows, width), jnp.bfloat16),
+            pltpu.VMEM((2, experts, width, rows), jnp.bfloat16),
+            pltpu.VMEM((groups, 2, held, width), jnp.float32),
+            pltpu.VMEM((groups, n - 1, 2, held, width), jnp.float32),
+            pltpu.SemaphoreType.DMA((SLOTS, 2, 2)),
+            pltpu.SemaphoreType.DMA((2,)),
+            pltpu.SemaphoreType.DMA((2, n - 1)),
+            pltpu.SemaphoreType.DMA((2, n - 1)),
+            pltpu.SemaphoreType.DMA((n - 1,)),
+            pltpu.SemaphoreType.DMA((groups,)),
+        ],
+        compiler_params=pltpu.CompilerParams(
+            collective_id=0, has_side_effects=True, vmem_limit_bytes=56 * 2**20
+        ),
+    )(train_gate, other_gate, train_up, other_up)
+    mine = lax.dynamic_slice_in_dim(scales, lax.axis_index("zero") * piece, piece, axis=3)
+    mine = jnp.swapaxes(mine, 0, 1).reshape(2, experts, piece)
+    return jnp.swapaxes(ready_gate, 1, 2), jnp.swapaxes(ready_up, 1, 2), mine[0], mine[1]
+
+
+def weights_by_collectives(train_gate, other_gate, train_up, other_up):
     latest_gate = train_gate + other_gate.astype(jnp.float32)
     latest_up = train_up + other_up.astype(jnp.float32)
     scale_gate, scale_up = lax.pmax(
@@ -24,15 +189,27 @@
     scale_up = lax.dynamic_slice_in_dim(
         scale_up, lax.axis_index("zero") * ready_up.shape[2], ready_up.shape[2], axis=1
     )
+    return ready_gate, ready_up, scale_gate, scale_up
+
+
+def on_device(n, train_gate, other_gate, train_up, other_up, router_weight, router_gain):
     part_router = (router_weight * router_gain[:, None]).astype(jnp.bfloat16)
     row_router = lax.all_gather(part_router, "zero", axis=0, tiled=True)
     serve_router = lax.all_gather(row_router, "bank", axis=1, tiled=True)
-    return (ready_gate, ready_up, scale_gate, scale_up, serve_router)
+    experts, rows, width = train_gate.shape
+    held = 2 if experts % 2 == 0 else 1
+    whole_tiles = rows % LANES == 0 and width % LANES == 0 and (width // n) % 16 == 0
+    staged = 4 * experts * rows * width + SLOTS * held * 12 * rows * width
+    if n > 1 and whole_tiles and staged <= 48 * 2**20:
+        weights = weights_by_kernel(n, held, train_gate, other_gate, train_up, other_up)
+    else:
+        weights = weights_by_collectives(train_gate, other_gate, train_up, other_up)
+    return (*weights, serve_router)
 
 
 def solution(mesh):
     return jax.shard_map(
-        on_device,
+        functools.partial(on_device, mesh.shape["zero"]),
         mesh=mesh,
         in_specs=(
             P("bank", "zero", None),

time: 889 us -> 642 us (0.72)
  Pallas kernels: 0 us -> 578 us
  blocking collectives: 575 us -> 39.2 us
  local copies, waits for them, and re-layouts: 159 us -> 24 us
  waiting for transfers between devices: 78.2 us -> 0 us
  other arithmetic: 53.5 us -> 0.01 us
  between operations: 14.1 us -> 0.68 us
    pallas_call x0 -> x1, Pallas kernels: none -> 578 us  [weights_by_kernel(): pl.pallas_call(functools.partial(exchange, n, held), out_shape=(ready, re...]
    all_to_all x1 -> x0, blocking collectives: 276 us -> none  [on_device(): lax.all_to_all(narrow_gate, 'zero', split_axis=2, concat_axis=1, tiled=True)]
    all_gather x1, blocking collectives: 292 us -> 32 us  [on_device(): row_router = lax.all_gather(part_router, 'zero', axis=0, tiled=True)]
    pmax x1 -> x0, waiting for transfers between devices: 78.2 us -> none  [on_device(): lax.pmax((jnp.max(jnp.abs(latest_gate), axis=1), jnp.max(jnp.abs(latest_u...]
    unnamed x13 -> x7, local copies, waits for them, and re-layouts: 90.9 us -> 22.5 us
    all_to_all x4 -> x0, local copies, waits for them, and re-layouts: 67.1 us -> none  [the longest x2 33.5 us: on_device(): lax.all_to_all(narrow_gate, 'zero', split_axis=2, concat_axis=1, tiled=True)]
    convert_element_type x1 -> x0, other arithmetic: 29.4 us -> none  [on_device(): (latest_up / jnp.expand_dims(scale_up, 1)).astype(jnp.bfloat16)]
    reduce_max x2 -> x0, other arithmetic: 24.1 us -> none  [the longest x1 14.4 us: on_device(): jnp.max(jnp.abs(latest_up), axis=1)]
  transfers between devices with their start and end apart: 2 -> 0, of which waited for: 1 -> 0; matrix products, arithmetic and copies ran while one was open for 2% -> 0% of each run, Pallas kernels for 0% -> 0%
where the time goes in v1:
time: 642 us
  Pallas kernels  578 us (90%)
  blocking collectives  39.2 us (6%)
  local copies, waits for them, and re-layouts  24 us (4%)
    pallas_call x1, Pallas kernels, weights_by_kernel(): pl.pallas_call(functools.partial(exchange, n, held), out_shape=(ready, re...  578 us
    all_gather x1, blocking collectives, on_device(): row_router = lax.all_gather(part_router, 'zero', axis=0, tiled=True)  32 us
    unnamed x7, local copies, waits for them, and re-layouts  22.5 us

profile of v1, /device:TPU:0, one launch (start us, length us, event | category | flops | bytes accessed | tf_op | source)
XLA Modules:
  0.0 641.9 jit_solution(11443244065747981864)
XLA Ops:
  0.6 0.0 copy-start
  0.6 0.0 copy-start.1
  0.7 578.0 %shard_map.101 = (bf16[32,96,2048]{2,1,0:T(8,128)(2,1)}, bf16[32,96,2048]{2,1,0:T(8,128)(2,1)}, f32[16,2,2,768]{3,2,1,0:T(2,128)}) custom-call(f32[32,256,768]{2,1,0:T(8,128)} %train_gate.1, bf16[32,256,768]{2,1,0:T(8,128)(2,1)} %other_gate.1, f32[32,256,768]{2,1,0:T(8,128)} %train_up.1, bf16[32,256,768]{2,1,0:T(8,128)(2,1)} %other_up.1), custom_call_target="tpu_custom_call" | custom-call | tf_op jit(solution)/shard_map/pallas_call | solution.py:145
  578.6 0.9 dynamic-slice_bitcast_fusion
  579.6 0.6 fusion
  580.2 0.0 copy-done
  580.2 0.0 copy-done.1
  580.2 32.0 %all_gather.6 = bf16[2048,32]{0,1:T(8,128)(2,1)S(1)} all-gather(bf16[256,32]{0,1:T(8,128)(2,1)S(1)} %multiply_convert_fusion), channel_id=1, replica_groups=mesh['bank'=4,'zero'=8] {'zero'}, dimensions={0}, use_global_device_ids=true | all-gather | bytes 147456 | tf_op jit(solution)/shard_map/all_gather | solution.py:197
  612.2 7.2 %all_gather.7 = bf16[2048,128]{0,1:T(8,128)(2,1)S(1)} all-gather(bf16[2048,32]{0,1:T(8,128)(2,1)S(1)} %all_gather.6), channel_id=1, replica_groups=mesh['bank'=4,'zero'=8] {'bank'}, dimensions={1}, use_global_device_ids=true | all-gather | bytes 655360 | tf_op jit(solution)/shard_map/all_gather | solution.py:198
  619.4 1.0 copy.12
  620.4 10.7 %copy.15 = bf16[32,2048,96]{1,2,0:T(8,128)(2,1)} copy(bf16[32,2048,96]{1,2,0:T(8,128)(2,1)} %bitcast.7) | data formatting | bytes 25165824
  631.1 10.7 %copy.16 = bf16[32,2048,96]{1,2,0:T(8,128)(2,1)} copy(bf16[32,2048,96]{1,2,0:T(8,128)(2,1)} %bitcast.6) | data formatting | bytes 25165824
  (1 shorter events, 0.0 us)
Async XLA Ops:
  0.6 579.6 %copy-start = (f32[256,32]{0,1:T(8,128)S(1)}, f32[256,32]{0,1:T(8,128)}, u32[]{:S(2)}) copy-start(f32[256,32]{0,1:T(8,128)} %param.10) | copy-start | bytes 98308
  0.6 579.5 %copy-start.1 = (f32[256]{0:T(256)S(1)}, f32[256]{0:T(256)}, u32[]{:S(2)}) copy-start(f32[256]{0:T(256)} %param.11) | copy-start | bytes 3076
